TPU v7x, 32 devices: a whole 2x2x4 slice. The times are simulated.
32 devices in a mesh: row: 8 (over y, x, core), col: 4 (over z).
Axes of the slice: x: 2, y: 2, z: 4, core: 2. Of those that a mesh axis runs over, the one named last changes fastest.
Arguments:
- matrix: float32 [16384, 8192], P('row', 'col'), may hold values from -40 to 40
Outputs:
- upper: float32 [256, 8192], P('row', 'col')
- reduced: float32 [16384, 8192], P('row', 'col')
All inputs are finite; a program needn't handle non-finite values.
Results may differ from a plain program's by a relative error of at most 0.0003.
Values sent between devices are 32-bit elements; how exact they have to be, the bound alone decides.
A program may use at most 128 MiB of HBM per device.

v0:
```python
import jax
import jax.numpy as jnp
from jax import lax
from jax.sharding import PartitionSpec as P

PANEL = 256
precise = lax.Precision.HIGHEST


def broadcast(shard, axis, root):
    mine = lax.axis_index(axis) == root
    return lax.psum(jnp.where(mine, shard, jnp.zeros_like(shard)), axis)


def multiply(left, right):
    return jnp.dot(left, right, precision=precise, preferred_element_type=jnp.float32)


def cholesky_pass(block):
    gram = multiply(block.T, block)
    lower = jnp.linalg.cholesky(gram)
    basis = jax.scipy.linalg.solve_triangular(lower, block.T, lower=True).T
    return (basis, lower.T)


def factorize(block):
    first_basis, first_upper = cholesky_pass(block)
    second_basis, second_upper = cholesky_pass(first_basis)
    return (second_basis, multiply(second_upper, first_upper))


def shards(matrix):
    row_count = lax.axis_size("row")
    total_rows = matrix.shape[0] * row_count
    share_rows = PANEL // row_count
    panel = matrix[:, :PANEL]
    local_basis, local_upper = factorize(panel)
    total_gram = lax.psum(multiply(local_upper.T, local_upper), "row")
    whole_upper = jnp.linalg.cholesky(total_gram).T
    change = jax.scipy.linalg.solve_triangular(whole_upper.T, local_upper.T, lower=True).T
    basis = multiply(local_basis, change)
    basis = broadcast(basis, "col", 0)
    full_upper = lax.psum(multiply(basis.T, matrix), "row")
    my_share = lax.dynamic_slice_in_dim(
        full_upper, lax.axis_index("row") * share_rows, share_rows, 0
    )
    projected = matrix - multiply(basis, full_upper)
    scale = jnp.sqrt(jnp.float32(total_rows))
    placed = jnp.concatenate([basis * scale, projected[:, PANEL:]], axis=1)
    reduced = jnp.where(lax.axis_index("col") == 0, placed, projected)
    return (my_share, reduced)


def solution(mesh):
    return jax.shard_map(
        shards,
        mesh=mesh,
        in_specs=(P("row", "col"),),
        out_specs=(P("row", "col"), P("row", "col")),
        check_vma=False,
    )
```

profile of v0, /device:TPU:8, one launch (start us, length us, event | category | flops | bytes accessed | tf_op | source)
XLA Modules:
  0.0 487.8 jit_solution(14583731544222165822)
XLA Ops:
  7.2 5.7 %fusion.7 = f32[256,256]{1,0:T(8,128)S(1)} fusion(f32[2048,2048]{1,0:T(8,128)} %param.4), kind=kOutput, calls=%fused_computation.19 | convolution fusion | flops 1610612736 | bytes 2359296 | tf_op jit(solution)/shard_map/dot_general | solution.py:16
  12.9 3.0 slice_bitcast_fusion
  16.2 11.7 %cholesky.172 = f32[128,128]{1,0:T(8,128)S(1)} custom-call(f32[128,128]{1,0:T(8,128)S(1)} %cholesky.270), custom_call_target="Cholesky" | custom-call | tf_op jit(solution)/shard_map/jit(cholesky)/cholesky | solution.py:21
  27.9 9.8 %custom-call.19 = f32[1,128,128]{1,2,0:T(8,128)S(1)} custom-call(f32[1,128,128]{2,1,0:T(8,128)S(1)} %get-tuple-element.71), custom_call_target="InvertDiagBlocksLowerTriangular" | custom-call | tf_op jit(solution)/shard_map/jit(cholesky)/cholesky | solution.py:21
  38.2 11.9 %cholesky.189 = f32[128,128]{1,0:T(8,128)S(1)} custom-call(f32[128,128]{1,0:T(8,128)S(1)} %convolution_subtract_fusion.6), custom_call_target="Cholesky" | custom-call | tf_op jit(solution)/shard_map/jit(cholesky)/cholesky | solution.py:21
  50.2 0.7 compare_reduce_fusion.4
  52.3 4.1 while.6
  53.0 1.3 bitcast_dynamic-update-slice_fusion.7
  55.0 1.3 bitcast_dynamic-update-slice_fusion.7
  56.4 19.7 %custom-call.20 = f32[2,128,128]{1,2,0:T(8,128)S(1)} custom-call(f32[2,128,128]{2,1,0:T(8,128)S(1)} %get-tuple-element.26), custom_call_target="InvertDiagBlocksLowerTriangular" | custom-call | tf_op jit(solution)/shard_map/jit(_solve_triangular)/triangular_solve | solution.py:22
  76.1 2.3 fusion.9
  78.3 3.0 convolution_subtract_fusion.2
  81.4 1.1 fusion.40
  82.5 1.9 fusion
  84.5 11.7 %cholesky.206 = f32[128,128]{1,0:T(8,128)S(1)} custom-call(f32[128,128]{1,0:T(8,128)S(1)} %cholesky.273), custom_call_target="Cholesky" | custom-call | tf_op jit(solution)/shard_map/jit(cholesky)/cholesky | solution.py:21
  96.9 10.2 %custom-call.21 = f32[1,128,128]{1,2,0:T(8,128)S(1)} custom-call(f32[1,128,128]{2,1,0:T(8,128)S(1)} %get-tuple-element.67), custom_call_target="InvertDiagBlocksLowerTriangular" | custom-call | tf_op jit(solution)/shard_map/jit(cholesky)/cholesky | solution.py:21
  107.6 11.7 %cholesky.223 = f32[128,128]{1,0:T(8,128)S(1)} custom-call(f32[128,128]{1,0:T(8,128)S(1)} %convolution_subtract_fusion.5), custom_call_target="Cholesky" | custom-call | tf_op jit(solution)/shard_map/jit(cholesky)/cholesky | solution.py:21
  121.8 1.3 fusion.57
  123.3 4.0 while.7
  124.0 1.3 bitcast_dynamic-update-slice_fusion.8
  126.0 1.3 bitcast_dynamic-update-slice_fusion.8
  128.0 19.8 %custom-call.22 = f32[2,128,128]{1,2,0:T(8,128)S(1)} custom-call(f32[2,128,128]{2,1,0:T(8,128)S(1)} %get-tuple-element.27), custom_call_target="InvertDiagBlocksLowerTriangular" | custom-call | tf_op jit(solution)/shard_map/jit(_solve_triangular)/triangular_solve | solution.py:22
  147.9 1.1 fusion.36
  148.9 1.9 convolution_subtract_fusion.1
  150.8 1.1 fusion.35
  151.9 26.7 %all-reduce.5.cloned.1.call-done = f32[256,256]{0,1:T(8,128)} async-done(((f32[256,256]{0,1:T(8,128)}), f32[256,256]{0,1:T(8,128)}) %all-reduce.5.cloned.1.call-update) | async-done | bytes 262160 | tf_op jit(solution)/shard_map/psum | solution.py:38
  178.6 1.1 copy.6
  179.7 1.0 fusion.14
  180.7 11.7 %cholesky.240 = f32[128,128]{1,0:T(8,128)S(1)} custom-call(f32[128,128]{1,0:T(8,128)S(1)} %cholesky.276), custom_call_target="Cholesky" | custom-call | tf_op jit(solution)/shard_map/jit(cholesky)/cholesky | solution.py:39
  193.1 9.8 %custom-call.23 = f32[1,128,128]{1,2,0:T(8,128)S(1)} custom-call(f32[1,128,128]{2,1,0:T(8,128)S(1)} %get-tuple-element.63), custom_call_target="InvertDiagBlocksLowerTriangular" | custom-call | tf_op jit(solution)/shard_map/jit(cholesky)/cholesky | solution.py:39
  203.4 11.9 %cholesky.257 = f32[128,128]{1,0:T(8,128)S(1)} custom-call(f32[128,128]{1,0:T(8,128)S(1)} %convolution_subtract_fusion.4), custom_call_target="Cholesky" | custom-call | tf_op jit(solution)/shard_map/jit(cholesky)/cholesky | solution.py:39
  215.3 0.7 compare_reduce_fusion
  217.5 4.1 while.5
  218.1 1.4 bitcast_dynamic-update-slice_fusion.6
  220.1 1.4 bitcast_dynamic-update-slice_fusion.6
  221.6 19.7 %custom-call.15 = f32[2,128,128]{1,2,0:T(8,128)S(1)} custom-call(f32[2,128,128]{2,1,0:T(8,128)S(1)} %get-tuple-element.19), custom_call_target="InvertDiagBlocksLowerTriangular" | custom-call | tf_op jit(solution)/shard_map/jit(_solve_triangular)/triangular_solve | solution.py:40
  242.3 4.8 convolution_select_fusion
  247.1 84.5 %all-reduce.7.cloned.1.call-done = f32[2048,256]{1,0:T(8,128)} async-done(((f32[2048,256]{1,0:T(8,128)}), f32[2048,256]{1,0:T(8,128)}) %all-reduce.7.cloned.1.call-update) | async-done | bytes 2097168 | tf_op jit(solution)/shard_map/psum | solution.py:12
  331.7 18.6 %fusion.58 = f32[256,2048]{1,0:T(8,128)} fusion(f32[2048,256]{1,0:T(8,128)} %all-reduce.7.cloned.1.call-done, f32[2048,2048]{1,0:T(8,128)} %param.4), kind=kOutput, calls=%fused_computation.107 | convolution fusion | flops 12884901888 | bytes 20971520 | tf_op jit(solution)/shard_map/dot_general | solution.py:16
  350.3 17.9 %copy.7 = f32[2048,2048]{0,1:T(8,128)} copy(f32[2048,2048]{1,0:T(8,128)} %param.4) | data formatting | bytes 33554432 | tf_op args[0]
  368.1 1.5 broadcast_multiply_fusion
  369.6 2.9 copy.8
  372.5 39.7 %all-reduce.9.cloned.1.call-done = f32[256,2048]{1,0:T(8,128)} async-done(((f32[256,2048]{1,0:T(8,128)}), f32[256,2048]{1,0:T(8,128)}) %all-reduce.9.cloned.1.call-update) | async-done | bytes 2097168 | tf_op jit(solution)/shard_map/psum | solution.py:43
  412.2 19.5 %convolution_subtract_fusion = f32[2048,2048]{0,1:T(8,128)} fusion(f32[2048,2048]{0,1:T(8,128)} %copy.7, f32[2048,256]{1,0:T(8,128)S(1)} %copy-done, f32[256,2048]{1,0:T(8,128)} %all-reduce.9.cloned.1.call-done), kind=kOutput, calls=%fused_computation.7 | convolution fusion | flops 12889096192 | bytes 37748736 | tf_op jit(solution)/shard_map/dot_general | solution.py:16
  431.7 13.3 %slice.80 = f32[2048,1792]{0,1:T(8,128)} slice(f32[2048,2048]{0,1:T(8,128)} %convolution_subtract_fusion), slice={[0:2048], [256:2048]} | slice | bytes 29360128 | tf_op jit(solution)/shard_map/slice | solution.py:49
  445.0 16.6 %maximum_select_fusion = f32[2048,2048]{0,1:T(8,128)} fusion(f32[2048,2048]{0,1:T(8,128)} %convolution_subtract_fusion, f32[2048,1792]{0,1:T(8,128)} %slice.80, f32[2048,256]{0,1:T(8,128)S(1)} %copy-done.1, pred[]{:T(512)S(6)} %eq.4), kind=kLoop, calls=%fused_computation.6 | loop fusion | flops 8388608 | bytes 50331648 | tf_op jit(solution)/shard_map/jit(_where)/select_n | solution.py:50
  461.5 17.6 %copy.9 = f32[2048,2048]{1,0:T(8,128)} copy(f32[2048,2048]{0,1:T(8,128)} %maximum_select_fusion) | data formatting | bytes 33554432
  479.1 1.7 constant_dynamic-slice_fusion.3
  (61 shorter events, 10.4 us)
Async XLA Ops:
  7.2 171.4 %all-reduce.5.cloned.1.call-start = ((), (), s32[]{:S(2)}) async-start(), calls=%async_computation | async-start | bytes 524288 | tf_op jit(solution)/shard_map/psum | solution.py:38
  123.2 208.5 %all-reduce.7.cloned.1.call-start = ((), (), s32[]{:S(2)}) async-start(), calls=%async_computation.1 | async-start | bytes 4194304 | tf_op jit(solution)/shard_map/psum | solution.py:12
  127.3 0.7 copy-start.2
  247.1 165.1 %all-reduce.9.cloned.1.call-start = ((), (), s32[]{:S(2)}) async-start(), calls=%async_computation.2 | async-start | bytes 4194304 | tf_op jit(solution)/shard_map/psum | solution.py:43
  350.3 17.9 %copy-start = (f32[2048,256]{1,0:T(8,128)S(1)}, f32[2048,256]{1,0:T(8,128)}, u32[]{:S(2)}) copy-start(f32[2048,256]{1,0:T(8,128)} %all-reduce.7.cloned.1.call-done) | copy-start | bytes 6291460
  431.7 13.3 %copy-start.1 = (f32[2048,256]{0,1:T(8,128)S(1)}, f32[2048,256]{0,1:T(8,128)}, u32[]{:S(2)}) copy-start(f32[2048,256]{0,1:T(8,128)} %copy.8) | copy-start | bytes 6291460
Sparse Core Ops, SparseCore 0:
  123.3 55.2 all-reduce.4
  247.2 84.4 all-reduce.6
  350.4 61.8 all-reduce.8
where the time goes:
time: 497 us; the launch traced here: 488 us
  other arithmetic  182 us (37%)
  waiting for transfers between devices  151 us (30%)
  local copies, waits for them, and re-layouts  70.6 us (14%)
  matrix products  64.9 us (13%)
  between operations  18.4 us (4%)
    psum x1, waiting for transfers between devices, broadcast(): return lax.psum(jnp.where(mine, shard, jnp.zeros_like(shard)), axis)  84.5 us
    another operation x13, other arithmetic, cholesky_pass(): lower = jnp.linalg.cholesky(gram)  69.2 us
    dot_general x7, matrix products, multiply(): jnp.dot(left, right, precision=precise, preferred_element_type=jnp.float32)  52.1 us
    psum x1, waiting for transfers between devices, shards(): full_upper = lax.psum(multiply(basis.T, matrix), 'row')  39.7 us
    another operation x5, other arithmetic, cholesky_pass(): basis = jax.scipy.linalg.solve_triangular(lower, block.T, lower=True).T  39.6 us
    unnamed x8, local copies, waits for them, and re-layouts  36.2 us
    another operation x7, other arithmetic, shards(): whole_upper = jnp.linalg.cholesky(total_gram).T  34.9 us
    psum x1, waiting for transfers between devices, shards(): total_gram = lax.psum(multiply(local_upper.T, local_upper), 'row')  26.7 us
  transfers between devices with their start and end apart: 3, of which 3 were waited for; matrix products, arithmetic and copies ran while one was open for 10% of the time, Pallas kernels for 0%

commit v1 on v0

--- a/solution.py
+++ b/solution.py
@@ -9,7 +9,7 @@
 
 def broadcast(shard, axis, root):
     mine = lax.axis_index(axis) == root
-    return lax.psum(jnp.where(mine, shard, jnp.zeros_like(shard)), axis)
+    return jnp.sum(lax.all_gather(jnp.where(mine, shard, jnp.zeros_like(shard)), axis), axis=0)
 
 
 def multiply(left, right):

time: 497 us -> 564 us (1.13)
  waiting for transfers between devices: 151 us -> 213 us
  other arithmetic: 182 us -> 188 us
    all_gather x0 -> x1, waiting for transfers between devices: none -> 146 us  [broadcast(): lax.all_gather(jnp.where(mine, shard, jnp.zeros_like(shard)), axis)]
    psum x1 -> x0, waiting for transfers between devices: 84.5 us -> none  [broadcast(): return lax.psum(jnp.where(mine, shard, jnp.zeros_like(shard)), axis)]
    unnamed x8 -> x6, local copies, waits for them, and re-layouts: 36.2 us -> 36.1 us
  transfers between devices with their start and end apart: 3 -> 3, of which waited for: 3 -> 3; matrix products, arithmetic and copies ran while one was open for 10% -> 9% of each run, Pallas kernels for 0% -> 0%
where the time goes in v1:
time: 564 us; the launch traced here: 554 us
  waiting for transfers between devices  213 us (38%)
  other arithmetic  188 us (33%)
  local copies, waits for them, and re-layouts  69.4 us (12%)
  matrix products  64.3 us (11%)
  between operations  18.4 us (3%)
    all_gather x1, waiting for transfers between devices, broadcast(): lax.all_gather(jnp.where(mine, shard, jnp.zeros_like(shard)), axis)  146 us
    another operation x13, other arithmetic, cholesky_pass(): lower = jnp.linalg.cholesky(gram)  69.2 us
    dot_general x7, matrix products, multiply(): jnp.dot(left, right, precision=precise, preferred_element_type=jnp.float32)  51.6 us
    psum x1, waiting for transfers between devices, shards(): full_upper = lax.psum(multiply(basis.T, matrix), 'row')  40.3 us
    another operation x5, other arithmetic, cholesky_pass(): basis = jax.scipy.linalg.solve_triangular(lower, block.T, lower=True).T  39.6 us
    unnamed x6, local copies, waits for them, and re-layouts  36.1 us
    another operation x7, other arithmetic, shards(): whole_upper = jnp.linalg.cholesky(total_gram).T  34.9 us
    psum x1, waiting for transfers between devices, shards(): total_gram = lax.psum(multiply(local_upper.T, local_upper), 'row')  26.7 us
  transfers between devices with their start and end apart: 3, of which 3 were waited for; matrix products, arithmetic and copies ran while one was open for 9% of the time, Pallas kernels for 0%

profile of v1, /device:TPU:8, one launch (start us, length us, event | category | flops | bytes accessed | tf_op | source)
XLA Modules:
  0.0 554.0 jit_solution(8036102069344924277)
XLA Ops:
  7.2 5.7 %fusion.7 = f32[256,256]{1,0:T(8,128)S(1)} fusion(f32[2048,2048]{1,0:T(8,128)} %param.4), kind=kOutput, calls=%fused_computation.19 | convolution fusion | flops 1610612736 | bytes 2359296 | tf_op jit(solution)/shard_map/dot_general | solution.py:16
  12.9 3.0 slice_bitcast_fusion
  16.2 11.7 %cholesky.172 = f32[128,128]{1,0:T(8,128)S(1)} custom-call(f32[128,128]{1,0:T(8,128)S(1)} %cholesky.270), custom_call_target="Cholesky" | custom-call | tf_op jit(solution)/shard_map/jit(cholesky)/cholesky | solution.py:21
  27.9 9.8 %custom-call.19 = f32[1,128,128]{1,2,0:T(8,128)S(1)} custom-call(f32[1,128,128]{2,1,0:T(8,128)S(1)} %get-tuple-element.73), custom_call_target="InvertDiagBlocksLowerTriangular" | custom-call | tf_op jit(solution)/shard_map/jit(cholesky)/cholesky | solution.py:21
  38.2 11.9 %cholesky.189 = f32[128,128]{1,0:T(8,128)S(1)} custom-call(f32[128,128]{1,0:T(8,128)S(1)} %convolution_subtract_fusion.6), custom_call_target="Cholesky" | custom-call | tf_op jit(solution)/shard_map/jit(cholesky)/cholesky | solution.py:21
  50.2 0.7 compare_reduce_fusion.4
  52.3 4.1 while.6
  53.0 1.3 bitcast_dynamic-update-slice_fusion.7
  55.0 1.3 bitcast_dynamic-update-slice_fusion.7
  56.4 19.7 %custom-call.20 = f32[2,128,128]{1,2,0:T(8,128)S(1)} custom-call(f32[2,128,128]{2,1,0:T(8,128)S(1)} %get-tuple-element.26), custom_call_target="InvertDiagBlocksLowerTriangular" | custom-call | tf_op jit(solution)/shard_map/jit(_solve_triangular)/triangular_solve | solution.py:22
  76.1 2.3 fusion.9
  78.3 3.0 convolution_subtract_fusion.2
  81.4 1.1 fusion.40
  82.5 1.9 fusion
  84.5 11.7 %cholesky.206 = f32[128,128]{1,0:T(8,128)S(1)} custom-call(f32[128,128]{1,0:T(8,128)S(1)} %cholesky.273), custom_call_target="Cholesky" | custom-call | tf_op jit(solution)/shard_map/jit(cholesky)/cholesky | solution.py:21
  96.9 10.2 %custom-call.21 = f32[1,128,128]{1,2,0:T(8,128)S(1)} custom-call(f32[1,128,128]{2,1,0:T(8,128)S(1)} %get-tuple-element.69), custom_call_target="InvertDiagBlocksLowerTriangular" | custom-call | tf_op jit(solution)/shard_map/jit(cholesky)/cholesky | solution.py:21
  107.6 11.7 %cholesky.223 = f32[128,128]{1,0:T(8,128)S(1)} custom-call(f32[128,128]{1,0:T(8,128)S(1)} %convolution_subtract_fusion.5), custom_call_target="Cholesky" | custom-call | tf_op jit(solution)/shard_map/jit(cholesky)/cholesky | solution.py:21
  121.8 1.3 fusion.57
  123.3 4.0 while.7
  124.0 1.3 bitcast_dynamic-update-slice_fusion.8
  126.0 1.3 bitcast_dynamic-update-slice_fusion.8
  128.0 19.8 %custom-call.22 = f32[2,128,128]{1,2,0:T(8,128)S(1)} custom-call(f32[2,128,128]{2,1,0:T(8,128)S(1)} %get-tuple-element.27), custom_call_target="InvertDiagBlocksLowerTriangular" | custom-call | tf_op jit(solution)/shard_map/jit(_solve_triangular)/triangular_solve | solution.py:22
  147.9 1.1 fusion.36
  148.9 1.9 convolution_subtract_fusion.1
  150.8 1.1 fusion.35
  151.9 26.7 %all-reduce.4.cloned.1.call-done = f32[256,256]{0,1:T(8,128)} async-done(((f32[256,256]{0,1:T(8,128)}), f32[256,256]{0,1:T(8,128)}) %all-reduce.4.cloned.1.call-update) | async-done | bytes 262160 | tf_op jit(solution)/shard_map/psum | solution.py:38
  178.6 1.1 copy.12
  179.7 1.0 fusion.14
  180.7 11.7 %cholesky.240 = f32[128,128]{1,0:T(8,128)S(1)} custom-call(f32[128,128]{1,0:T(8,128)S(1)} %cholesky.276), custom_call_target="Cholesky" | custom-call | tf_op jit(solution)/shard_map/jit(cholesky)/cholesky | solution.py:39
  193.1 9.8 %custom-call.23 = f32[1,128,128]{1,2,0:T(8,128)S(1)} custom-call(f32[1,128,128]{2,1,0:T(8,128)S(1)} %get-tuple-element.65), custom_call_target="InvertDiagBlocksLowerTriangular" | custom-call | tf_op jit(solution)/shard_map/jit(cholesky)/cholesky | solution.py:39
  203.4 11.9 %cholesky.257 = f32[128,128]{1,0:T(8,128)S(1)} custom-call(f32[128,128]{1,0:T(8,128)S(1)} %convolution_subtract_fusion.4), custom_call_target="Cholesky" | custom-call | tf_op jit(solution)/shard_map/jit(cholesky)/cholesky | solution.py:39
  217.5 4.1 while.5
  218.1 1.4 bitcast_dynamic-update-slice_fusion.6
  220.1 1.4 bitcast_dynamic-update-slice_fusion.6
  221.6 19.7 %custom-call.15 = f32[2,128,128]{1,2,0:T(8,128)S(1)} custom-call(f32[2,128,128]{2,1,0:T(8,128)S(1)} %get-tuple-element.19), custom_call_target="InvertDiagBlocksLowerTriangular" | custom-call | tf_op jit(solution)/shard_map/jit(_solve_triangular)/triangular_solve | solution.py:40
  242.3 4.8 convolution_select_fusion
  247.1 146.2 %all-gather.3.cloned.1.call-done = f32[8192,256]{1,0:T(8,128)} async-done(((f32[2048,256]{1,0:T(8,128)}), f32[8192,256]{1,0:T(8,128)}) %all-gather.3.cloned.1.call-update) | async-done | bytes 8388624 | tf_op jit(solution)/shard_map/all_gather | solution.py:12
  393.3 4.2 reduce_sum.9
  397.5 18.0 %fusion.58 = f32[256,2048]{1,0:T(8,128)} fusion(f32[2048,256]{1,0:T(8,128)S(1)} %reduce_sum.9, f32[2048,2048]{1,0:T(8,128)} %param.4), kind=kOutput, calls=%fused_computation.107 | convolution fusion | flops 12884901888 | bytes 20971520 | tf_op jit(solution)/shard_map/dot_general | solution.py:16
  415.5 17.8 %copy.14 = f32[2048,2048]{0,1:T(8,128)} copy(f32[2048,2048]{1,0:T(8,128)} %param.4) | data formatting | bytes 33554432 | tf_op args[0]
  433.3 1.8 copy.13
  435.1 3.1 broadcast_multiply_fusion
  438.2 40.3 %all-reduce.6.cloned.1.call-done = f32[256,2048]{1,0:T(8,128)} async-done(((f32[256,2048]{1,0:T(8,128)}), f32[256,2048]{1,0:T(8,128)}) %all-reduce.6.cloned.1.call-update) | async-done | bytes 2097168 | tf_op jit(solution)/shard_map/psum | solution.py:43
  478.5 19.4 %convolution_subtract_fusion = f32[2048,2048]{0,1:T(8,128)} fusion(f32[2048,2048]{0,1:T(8,128)} %copy.14, f32[2048,256]{1,0:T(8,128)S(1)} %reduce_sum.9, f32[256,2048]{1,0:T(8,128)} %all-reduce.6.cloned.1.call-done), kind=kOutput, calls=%fused_computation.7 | convolution fusion | flops 12889096192 | bytes 37748736 | tf_op jit(solution)/shard_map/dot_general | solution.py:16
  498.0 13.3 %slice.80 = f32[2048,1792]{0,1:T(8,128)} slice(f32[2048,2048]{0,1:T(8,128)} %convolution_subtract_fusion), slice={[0:2048], [256:2048]} | slice | bytes 29360128 | tf_op jit(solution)/shard_map/slice | solution.py:49
  511.2 16.6 %maximum_select_fusion = f32[2048,2048]{0,1:T(8,128)} fusion(f32[2048,2048]{0,1:T(8,128)} %convolution_subtract_fusion, f32[2048,1792]{0,1:T(8,128)} %slice.80, f32[2048,256]{0,1:T(8,128)S(1)} %copy-done, pred[]{:T(512)S(6)} %eq.4), kind=kLoop, calls=%fused_computation.6 | loop fusion | flops 8388608 | bytes 50331648 | tf_op jit(solution)/shard_map/jit(_where)/select_n | solution.py:50
  527.8 17.6 %copy.15 = f32[2048,2048]{1,0:T(8,128)} copy(f32[2048,2048]{0,1:T(8,128)} %maximum_select_fusion) | data formatting | bytes 33554432
  545.4 1.7 constant_dynamic-slice_fusion.3
  (60 shorter events, 11.1 us)
Async XLA Ops:
  7.2 171.4 %all-reduce.4.cloned.1.call-start = ((), (), s32[]{:S(2)}) async-start(), calls=%async_computation | async-start | bytes 524288 | tf_op jit(solution)/shard_map/psum | solution.py:38
  123.2 270.1 %all-gather.3.cloned.1.call-start = ((), (), s32[]{:S(2)}) async-start(), calls=%async_computation.2 | async-start | bytes 10485760 | tf_op jit(solution)/shard_map/all_gather | solution.py:12
  127.3 0.7 copy-start.1
  247.1 231.4 %all-reduce.6.cloned.1.call-start = ((), (), s32[]{:S(2)}) async-start(), calls=%async_computation.1 | async-start | bytes 4194304 | tf_op jit(solution)/shard_map/psum | solution.py:43
  497.9 13.3 %copy-start = (f32[2048,256]{0,1:T(8,128)S(1)}, f32[2048,256]{0,1:T(8,128)}, u32[]{:S(2)}) copy-start(f32[2048,256]{0,1:T(8,128)} %broadcast_multiply_fusion) | copy-start | bytes 6291460
Sparse Core Ops, SparseCore 0:
  123.3 55.2 all-reduce.3
  247.2 146.0 all-gather.2
  415.6 62.8 all-reduce.5
